TPU v7x, 32 devices: a whole 2x2x4 slice. The times are simulated.
32 devices in a mesh: rows: 8 (over z, y), cols: 4 (over x, core).
Axes of the slice: x: 2, y: 2, z: 4, core: 2. Of those that a mesh axis runs over, the one named last changes fastest.
Arguments:
- gradient: float32 [8192, 29568], P('rows', 'cols'), as said below
- start_block: float32 [29568, 64], P('cols'), may hold values from -0.03125 to 0.03125
- activations: float32 [512, 29568], P('rows', 'cols'), may hold values from -6 to 6
- out_grads: float32 [512, 8192], P('rows', 'cols'), may hold values from -6 to 6
Outputs:
- left_factor: float32 [8192, 64], P('rows')
- right_factor: float32 [29568, 64], P('cols')
- scores: float32 [512], P('rows')
Inputs may be any that keep to these rules, and one draw needn't show every extreme that they name: real-valued gradient entries, of order 29568 ** -0.5.
All inputs are finite; a program needn't handle non-finite values.
Results may differ from a plain program's by a relative error of at most 0.00013.
Values sent between devices are 32-bit elements; how exact they have to be, the bound alone decides.
A program may use at most 128 MiB of HBM per device.

v0:
```python
import jax
import jax.numpy as jnp
from jax import lax
from jax.sharding import PartitionSpec as P

ITERS = 2


HIGH = lax.Precision.HIGHEST


def factor_with(block, gram):
    lower = jnp.linalg.cholesky(gram)
    return (
        lax.linalg.triangular_solve(lower, block, left_side=False, lower=True, transpose_a=True),
        lower,
    )


def inner_gram(block):
    return jnp.dot(block.T, block, precision=HIGH, preferred_element_type=jnp.float32)


def per_device(gradient, start_block, activations, out_grads):
    grad_cols = out_grads.shape[1]
    col_index = lax.axis_index("cols")
    omega = start_block
    for step in range(ITERS):
        ysum = lax.psum(
            jnp.dot(gradient, omega, precision=HIGH, preferred_element_type=jnp.float32), "cols"
        )
        gram = lax.psum(inner_gram(ysum), "rows")
        left, lower_y = factor_with(ysum, gram)
        partial_z = jnp.dot(gradient.T, left, precision=HIGH, preferred_element_type=jnp.float32)
        zsum = lax.psum(partial_z, "rows")
        zgram = lax.psum(inner_gram(zsum), "cols")
        right, lower_z = factor_with(zsum, zgram)
        omega = right
    whole_rows = lax.all_gather(left, "rows", axis=0, tiled=True)
    left_cols = lax.dynamic_slice_in_dim(whole_rows, col_index * grad_cols, grad_cols, 0)
    left_part = jnp.dot(out_grads, left_cols, precision=HIGH, preferred_element_type=jnp.float32)
    right_part = jnp.dot(activations, right, precision=HIGH, preferred_element_type=jnp.float32)
    token_left, token_right = lax.psum((left_part, right_part), "cols")
    mixed = jnp.dot(token_left, lower_z, precision=HIGH, preferred_element_type=jnp.float32)
    scores = jnp.sum(mixed * token_right, axis=1)
    return (left, right, scores)


def solution(mesh):
    placed = (P("rows", "cols"), P("cols", None), P("rows", "cols"), P("rows", "cols"))
    return jax.shard_map(
        per_device,
        mesh=mesh,
        in_specs=placed,
        out_specs=(P("rows", None), P("cols", None), P("rows")),
        check_vma=False,
    )
```

profile of v0, /device:TPU:0, one launch (start us, length us, event | category | flops | bytes accessed | tf_op | source)
XLA Modules:
  0.0 579.3 jit_solution(6776016720726716855)
XLA Ops:
  7.2 1.5 copy-done
  8.7 24.2 %fusion.23 = f32[1024,64]{0,1:T(8,128)} fusion(f32[1024,7392]{0,1:T(8,128)} %param.9, f32[7392,64]{0,1:T(8,128)S(1)} %copy-done), kind=kOutput, calls=%fused_computation.50 | convolution fusion | flops 5813305344 | bytes 32432128 | tf_op jit(solution)/shard_map/dot_general | solution.py:30
  33.0 35.1 %all-reduce.6.cloned.1.call-done = f32[1024,64]{0,1:T(8,128)} async-done(((f32[1024,64]{0,1:T(8,128)}), f32[1024,64]{0,1:T(8,128)}) %all-reduce.6.cloned.1.call-update) | async-done | bytes 262160 | tf_op jit(solution)/shard_map/psum | solution.py:29
  68.1 1.4 fusion.24
  69.5 37.7 %psum.71 = f32[64,64]{0,1:T(8,128)S(1)} all-reduce(f32[64,64]{0,1:T(8,128)S(1)} %fusion.24), channel_id=1, replica_groups=mesh['rows'=8,'cols'=4] {'rows'}, use_global_device_ids=true, to_apply=%region_1.0 | all-reduce | flops 4096 | bytes 32768 | tf_op jit(solution)/shard_map/psum | solution.py:32
  107.2 0.1 copy.8
  107.3 5.8 %cholesky.74 = f32[64,64]{1,0:T(8,128)S(1)} custom-call(f32[64,64]{1,0:T(8,128)S(1)} %fusion.12), custom_call_target="Cholesky" | custom-call | tf_op jit(solution)/shard_map/jit(cholesky)/cholesky | solution.py:13
  113.2 0.6 compare_reduce_fusion.3
  113.9 0.7 fusion.2
  114.5 4.9 custom-call.10
  119.4 1.4 convolution_bitcast_fusion.5
  120.8 30.9 %convolution_bitcast_fusion.3 = f32[7392,64]{0,1:T(8,128)} fusion(f32[1024,64]{0,1:T(8,128)S(1)} %convolution_bitcast_fusion.5, f32[1024,7392]{0,1:T(8,128)} %param.9), kind=kOutput, calls=%fused_computation.3 | convolution fusion | flops 5813305344 | bytes 32432128 | tf_op jit(solution)/shard_map/dot_general | solution.py:34
  151.8 93.5 %all-reduce.8.cloned.1.call-done = f32[7392,64]{0,1:T(8,128)} async-done(((f32[7392,64]{0,1:T(8,128)}), f32[7392,64]{0,1:T(8,128)}) %all-reduce.8.cloned.1.call-update) | async-done | bytes 1892368 | tf_op jit(solution)/shard_map/psum | solution.py:35
  245.3 3.8 fusion.25
  249.0 11.6 %psum.73 = f32[64,64]{0,1:T(8,128)S(1)} all-reduce(f32[64,64]{0,1:T(8,128)S(1)} %fusion.25), channel_id=1, replica_groups=mesh['rows'=8,'cols'=4] {'cols'}, use_global_device_ids=true, to_apply=%region_5.8 | all-reduce | flops 4096 | bytes 32768 | tf_op jit(solution)/shard_map/psum | solution.py:36
  260.6 0.1 copy.10
  260.7 5.8 %cholesky.85 = f32[64,64]{1,0:T(8,128)S(1)} custom-call(f32[64,64]{1,0:T(8,128)S(1)} %fusion.10), custom_call_target="Cholesky" | custom-call | tf_op jit(solution)/shard_map/jit(cholesky)/cholesky | solution.py:13
  266.6 0.6 compare_reduce_fusion.2
  267.2 0.7 fusion.3
  267.9 4.9 custom-call.11
  272.8 3.3 convolution_bitcast_fusion.2
  276.1 23.1 %convolution_bitcast_fusion.6 = f32[1024,64]{0,1:T(8,128)} fusion(f32[7392,64]{0,1:T(8,128)S(1)} %convolution_bitcast_fusion.2, f32[1024,7392]{0,1:T(8,128)} %param.9), kind=kOutput, calls=%fused_computation.6 | convolution fusion | flops 5813305344 | bytes 32432128 | tf_op jit(solution)/shard_map/dot_general | solution.py:30
  299.3 31.0 %all-reduce.10.cloned.1.call-done = f32[1024,64]{0,1:T(8,128)} async-done(((f32[1024,64]{0,1:T(8,128)}), f32[1024,64]{0,1:T(8,128)}) %all-reduce.10.cloned.1.call-update) | async-done | bytes 262160 | tf_op jit(solution)/shard_map/psum | solution.py:29
  330.3 1.4 fusion.26
  331.7 37.4 %psum.75 = f32[64,64]{0,1:T(8,128)S(1)} all-reduce(f32[64,64]{0,1:T(8,128)S(1)} %fusion.26), channel_id=1, replica_groups=mesh['rows'=8,'cols'=4] {'rows'}, use_global_device_ids=true, to_apply=%region_7.11 | all-reduce | flops 4096 | bytes 32768 | tf_op jit(solution)/shard_map/psum | solution.py:32
  369.1 0.1 copy.12
  369.2 5.8 %cholesky.96 = f32[64,64]{1,0:T(8,128)S(1)} custom-call(f32[64,64]{1,0:T(8,128)S(1)} %fusion.8), custom_call_target="Cholesky" | custom-call | tf_op jit(solution)/shard_map/jit(cholesky)/cholesky | solution.py:13
  375.1 0.6 compare_reduce_fusion.1
  375.7 0.7 fusion.4
  376.4 4.9 custom-call.12
  381.3 1.4 convolution_bitcast_fusion.4
  382.7 31.0 %convolution_bitcast_fusion.1 = f32[7392,64]{0,1:T(8,128)} fusion(f32[1024,64]{0,1:T(8,128)S(1)} %convolution_bitcast_fusion.4, f32[1024,7392]{0,1:T(8,128)} %param.9), kind=kOutput, calls=%fused_computation.1 | convolution fusion | flops 5813305344 | bytes 32432128 | tf_op jit(solution)/shard_map/dot_general | solution.py:34
  413.8 0.5 all-gather.2.cloned.1.call-update
  414.3 93.0 %all-reduce.12.cloned.1.call-done = f32[7392,64]{0,1:T(8,128)} async-done(((f32[7392,64]{0,1:T(8,128)}), f32[7392,64]{0,1:T(8,128)}) %all-reduce.12.cloned.1.call-update) | async-done | bytes 1892368 | tf_op jit(solution)/shard_map/psum | solution.py:35
  507.3 3.8 fusion.27
  511.1 11.7 %psum.77 = f32[64,64]{0,1:T(8,128)S(1)} all-reduce(f32[64,64]{0,1:T(8,128)S(1)} %fusion.27), channel_id=1, replica_groups=mesh['rows'=8,'cols'=4] {'cols'}, use_global_device_ids=true, to_apply=%region_9.13 | all-reduce | flops 4096 | bytes 32768 | tf_op jit(solution)/shard_map/psum | solution.py:36
  522.8 0.1 copy.14
  522.8 5.8 %cholesky.107 = f32[64,64]{1,0:T(8,128)S(1)} custom-call(f32[64,64]{1,0:T(8,128)S(1)} %fusion.6), custom_call_target="Cholesky" | custom-call | tf_op jit(solution)/shard_map/jit(cholesky)/cholesky | solution.py:13
  528.7 0.6 compare_reduce_fusion
  529.4 0.6 select_bitcast_fusion
  529.9 4.9 custom-call.13
  534.9 3.4 convolution_bitcast_fusion
  538.3 1.2 copy-done.1
  539.5 1.7 convolution_bitcast_fusion.7
  541.2 17.6 %all-gather.2.cloned.1.call-done = f32[8192,64]{0,1:T(8,128)} async-done(((f32[1024,64]{0,1:T(8,128)}), f32[8192,64]{0,1:T(8,128)}) %all-gather.2.cloned.1.call-update) | async-done | bytes 2097168 | tf_op jit(solution)/shard_map/all_gather | solution.py:39
  558.8 1.6 convolution_bitcast_fusion.8
  560.4 10.7 %all-reduce = (f32[64,64]{0,1:T(8,128)S(1)}, f32[64,64]{0,1:T(8,128)S(1)}) all-reduce(f32[64,64]{0,1:T(8,128)S(1)} %convolution_bitcast_fusion.7, f32[64,64]{0,1:T(8,128)S(1)} %convolution_bitcast_fusion.8), channel_id=1, replica_groups=mesh['rows'=8,'cols'=4] {'cols'}, use_global_device_ids=true, to_apply=%region_11.15 | all-reduce | flops 8192 | bytes 65536 | tf_op jit(solution)/shard_map/psum | solution.py:43
  571.1 1.3 fusion
  (25 shorter events, 0.5 us)
Async XLA Ops:
  7.2 1.5 copy-start
  7.2 60.9 %all-reduce.6.cloned.1.call-start = ((), (), s32[]{:S(2)}) async-start(), calls=%async_computation | async-start | bytes 524288 | tf_op jit(solution)/shard_map/psum | solution.py:29
  32.9 212.4 %all-reduce.8.cloned.1.call-start = ((), (), s32[]{:S(2)}) async-start(), calls=%async_computation.1 | async-start | bytes 3801088 | tf_op jit(solution)/shard_map/psum | solution.py:35
  151.7 178.6 %all-reduce.10.cloned.1.call-start = ((), (), s32[]{:S(2)}) async-start(), calls=%async_computation.2 | async-start | bytes 524288 | tf_op jit(solution)/shard_map/psum | solution.py:29
  299.2 208.1 %all-reduce.12.cloned.1.call-start = ((), (), s32[]{:S(2)}) async-start(), calls=%async_computation.3 | async-start | bytes 3801088 | tf_op jit(solution)/shard_map/psum | solution.py:35
  382.7 31.0 %copy-start.2 = (f32[1024,64]{0,1:T(8,128)}, f32[1024,64]{0,1:T(8,128)S(1)}, u32[]{:S(2)}) copy-start(f32[1024,64]{0,1:T(8,128)S(1)} %convolution_bitcast_fusion.4) | copy-start | bytes 786436
  413.7 145.1 %all-gather.2.cloned.1.call-start = ((), (), s32[]{:S(2)}) async-start(), calls=%async_computation.4 | async-start | bytes 2359296 | tf_op jit(solution)/shard_map/all_gather | solution.py:39
  534.9 4.7 copy-start.3
  538.3 1.3 copy-start.1
  539.5 19.3 %copy-start.4 = (f32[64,2048]{1,0:T(8,128)S(1)}, f32[64,2048]{1,0:T(8,128)}, u32[]{:S(2)}) copy-start(f32[64,2048]{1,0:T(8,128)} %param.12) | copy-start | bytes 1572868
Sparse Core Ops, SparseCore 0:
  33.0 35.0 all-reduce.5
  151.8 93.3 all-reduce.7
  299.3 30.9 all-reduce.9
  413.8 93.4 all-reduce.11
  509.9 48.8 all-gather.1
where the time goes:
time: 583 us; the launch traced here: 579 us
  waiting for transfers between devices  271 us (46%)
  matrix products  133 us (23%)
  blocking collectives  109 us (19%)
  other arithmetic  48.2 us (8%)
  between operations  14.3 us (2%)
    psum x2, waiting for transfers between devices, per_device(): zsum = lax.psum(partial_z, 'rows')  187 us
    psum x2, blocking collectives, per_device(): gram = lax.psum(inner_gram(ysum), 'rows')  75.2 us
    psum x2, waiting for transfers between devices, per_device(): lax.psum(jnp.dot(gradient, omega, precision=HIGH, preferred_element_type=...  66.2 us
    dot_general x2, matrix products, per_device(): jnp.dot(gradient.T, left, precision=HIGH, preferred_element_type=jnp.floa...  61.9 us
    dot_general x2, matrix products, per_device(): jnp.dot(gradient, omega, precision=HIGH, preferred_element_type=jnp.float32)  47.3 us
    another operation x12, other arithmetic, factor_with(): lower = jnp.linalg.cholesky(gram)  26.1 us
    psum x2, blocking collectives, per_device(): zgram = lax.psum(inner_gram(zsum), 'cols')  23.2 us
    another operation x8, other arithmetic, factor_with(): lax.linalg.triangular_solve(lower, block, left_side=False, lower=True, tr...  22.1 us
  transfers between devices with their start and end apart: 5, of which 5 were waited for; matrix products, arithmetic and copies ran while one was open for 4% of the time, Pallas kernels for 0%

commit v1 on v0

v1 whole, which is shorter than its diff:
```python
import functools

import jax
import jax.numpy as jnp
from jax import lax
from jax.experimental import pallas as pl
from jax.experimental.pallas import tpu as pltpu
from jax.sharding import PartitionSpec as P

ITERS = 2
HIGH = lax.Precision.HIGHEST
MESH = pl.DeviceIdType.MESH
F32 = jnp.float32
BF16 = jnp.bfloat16
CHUNK = 256
TILE = 64
SEGMENTS = 7
NT = (((1,), (1,)), ((), ()))
NN = (((1,), (0,)), ((), ()))


def dot(a, b, dims, precision=None):
    return lax.dot_general(a, b, dims, precision=precision, preferred_element_type=F32)


def split(x):
    hi = x.astype(BF16)
    return hi, (x - hi.astype(F32)).astype(BF16)


def chol_inverse(gram):
    n = gram.shape[0]
    sub = lax.broadcasted_iota(jnp.int32, (n, 2 * n), 0)
    lane = lax.broadcasted_iota(jnp.int32, (n, 2 * n), 1)
    eye = (lax.broadcasted_iota(jnp.int32, (n, n), 0) == lax.broadcasted_iota(jnp.int32, (n, n), 1)).astype(F32)
    w = jnp.concatenate([gram, eye], axis=1)
    for k in range(n):
        row = w[k : k + 1, :]
        scaled = row * (1.0 / row[:, k : k + 1])
        w = w - jnp.where(sub > k, w[:, k : k + 1], 0.0) * scaled
    diag = jnp.sum(jnp.where(sub == lane, w, 0.0), axis=1, keepdims=True)
    w = w * (1.0 / jnp.sqrt(diag))
    return w[:, :n], w[:, n:]


def pack(gram):
    half = gram.shape[0] // 2
    return jnp.concatenate([gram[:half], gram[half:]], axis=1)


def unpack(packed):
    n = packed.shape[1] // 2
    return jnp.concatenate([packed[:, :n], packed[:, n:]], axis=0)


def kernel(
    rows, cols, g_ref, w0_ref, left_ref, right_ref, core_ref,
    ghi, glo, fbuf, wcat, lcat, acc, ypart, yrecv, yfull, zpart, zpair, zgroup, zfull, gacc, grow, gcol,
    load_sem, ys_s, ys_r, ya_s, ya_r, gr_s, gr_r, gc_s, gc_r, p_s, p_r, q_s, q_r, a_s, a_r, b_s, b_r,
):
    r, c = lax.axis_index("rows"), lax.axis_index("cols")
    rank, wide = zfull.shape
    depth, n = g_ref.shape
    groups = rows // 2
    y, q = lax.rem(r, 2), lax.div(r, 2)
    half, eighth, quarter = rank // 2, rank // rows, rank // cols
    chunks = wide // CHUNK

    def load(t, slot):
        return pltpu.make_async_copy(
            g_ref.at[pl.ds(pl.multiple_of(t * TILE, TILE), TILE), :], fbuf.at[slot], load_sem.at[slot]
        )

    load(0, 0).start()

    barrier = pltpu.get_barrier_semaphore()
    for d in range(1, rows):
        pl.semaphore_signal(barrier, inc=1, device_id=(lax.rem(r + d, rows), c), device_id_type=MESH)
    for d in range(1, cols):
        pl.semaphore_signal(barrier, inc=1, device_id=(r, lax.rem(c + d, cols)), device_id_type=MESH)

    def put_factor(block, off):
        hi, lo = split(block)
        wcat[:rank, pl.ds(off, CHUNK)] = hi
        wcat[rank:, pl.ds(off, CHUNK)] = lo

    @pl.loop(0, chunks)
    def _(k):
        off = pl.multiple_of(k * CHUNK, CHUNK)
        put_factor(w0_ref[:, pl.ds(off, CHUNK)], off)

    ghi[:, wide - CHUNK :] = jnp.zeros((depth, CHUNK), BF16)
    glo[:, wide - CHUNK :] = jnp.zeros((depth, CHUNK), BF16)
    tiles = depth // TILE

    @pl.loop(0, tiles)
    def _(t):
        slot = lax.rem(t, 2)
        load(t, slot).wait()

        @pl.when(t + 1 < tiles)
        def _():
            load(t + 1, 1 - slot).start()

        hi, lo = split(fbuf[slot])
        at = pl.ds(pl.multiple_of(t * TILE, TILE), TILE)
        ghi[at, :n] = hi
        glo[at, :n] = lo

    pl.semaphore_wait(barrier, rows + cols - 2)

    def copy(src, dst, ssem, rsem, dev):
        cp = pltpu.make_async_remote_copy(
            src_ref=src, dst_ref=dst, send_sem=ssem, recv_sem=rsem, device_id=dev, device_id_type=MESH
        )
        cp.start()
        return cp

    def exchange(slots, me, count, ssem, rsem, device):
        cps = []
        for d in range(1, count):
            cps.append(copy(slots.at[me], slots.at[me], ssem.at[d - 1], rsem.at[d - 1], device(lax.rem(me + d, count))))
        for cp in cps:
            cp.wait()
        total = slots[0]
        for i in range(1, count):
            total = total + slots[i]
        return unpack(total)

    def rows_at(start, size):
        return pl.ds(pl.multiple_of(start, 8), size)

    bounds = [(chunks * s) // SEGMENTS for s in range(SEGMENTS + 1)]

    for step in range(ITERS):
        last = step == ITERS - 1
        acc[...] = jnp.zeros_like(acc)

        @pl.loop(0, chunks)
        def _(k):
            at = pl.ds(pl.multiple_of(k * CHUNK, CHUNK), CHUNK)
            w = wcat[:, at]
            acc[...] += dot(ghi[:, at], w, NT) + dot(glo[:, at], w, NT)

        for i in range(0, depth, 128):
            turned = acc[i : i + 128, :].T
            ypart[:, i : i + 128] = turned[:rank] + turned[rank:]
        cps = []
        for d in range(1, cols):
            p = lax.rem(c + d, cols)
            cps.append(copy(ypart.at[rows_at(p * quarter, quarter)], yrecv.at[d - 1], ys_s.at[d - 1], ys_r.at[d - 1], (r, p)))
        for cp in cps:
            cp.wait()
        own = rows_at(c * quarter, quarter)
        total = ypart[own, :]
        for d in range(1, cols):
            total = total + yrecv[d - 1]
        yfull[own, :] = total
        cps = []
        for d in range(1, cols):
            p = lax.rem(c + d, cols)
            cps.append(copy(yfull.at[own], yfull.at[own], ya_s.at[d - 1], ya_r.at[d - 1], (r, p)))
        for cp in cps:
            cp.wait()
        grow[r] = pack(dot(yfull[...], yfull[...], NT, HIGH))
        gram = exchange(grow, r, rows, gr_s, gr_r, lambda p: (p, c))
        _, inverse = chol_inverse(gram)
        left = dot(inverse, yfull[...], NN, HIGH)
        if last:
            left_ref[...] = left
        hi, lo = split(left)
        lcat[:rank, :] = hi
        lcat[rank:, :] = lo
        gacc[...] = jnp.zeros_like(gacc)
        flight = {}
        sends = []
        pair = (r + 1 - 2 * y, c)

        def start(key, cp):
            flight.setdefault(key, []).append(cp)
            sends.append(cp)

        def arrived(key):
            for cp in flight[key]:
                cp.wait_recv()

        def seg_at(s):
            return pl.ds(bounds[s] * CHUNK, (bounds[s + 1] - bounds[s]) * CHUNK)

        def stage0(s):
            @pl.loop(bounds[s], bounds[s + 1])
            def _(k):
                at = pl.ds(pl.multiple_of(k * CHUNK, CHUNK), CHUNK)
                part = dot(lcat[...], ghi[:, at], NN) + dot(lcat[...], glo[:, at], NN)
                zpart[:, at] = part[:rank] + part[rank:]

            other = rows_at((1 - y) * half, half)
            start(("p", s), copy(zpart.at[other, seg_at(s)], zpair.at[:, seg_at(s)], p_s.at[s], p_r.at[s], pair))

        def stage1(s):
            arrived(("p", s))
            at = seg_at(s)
            zpair[:, at] = zpair[:, at] + zpart[rows_at(y * half, half), at]
            for d in range(1, groups):
                p = lax.rem(q + d, groups)
                start(
                    ("q", s),
                    copy(
                        zpair.at[rows_at(p * eighth, eighth), at], zgroup.at[d - 1, :, at],
                        q_s.at[s, d - 1], q_r.at[s, d - 1], (2 * p + y, c),
                    ),
                )

        mine = rows_at(y * half + q * eighth, eighth)

        def stage2(s):
            arrived(("q", s))
            at = seg_at(s)
            total = zpair[rows_at(q * eighth, eighth), at]
            for d in range(1, groups):
                total = total + zgroup[d - 1, :, at]
            zfull[mine, at] = total
            for d in range(1, groups):
                p = lax.rem(q + d, groups)
                start(
                    ("a", s),
                    copy(zfull.at[mine, at], zfull.at[mine, at], a_s.at[s, d - 1], a_r.at[s, d - 1], (2 * p + y, c)),
                )

        def stage3(s):
            arrived(("a", s))
            at = seg_at(s)
            kept = rows_at(y * half, half)
            start(("b", s), copy(zfull.at[kept, at], zfull.at[kept, at], b_s.at[s], b_r.at[s], pair))

        def stage4(s):
            arrived(("b", s))
            block = zfull[:, seg_at(s)]
            gacc[...] += dot(block, block, NT, HIGH)

        stages = (stage0, stage1, stage2, stage3, stage4)
        for tick in range(SEGMENTS + len(stages) - 1):
            for i, stage in enumerate(stages):
                if 0 <= tick - i < SEGMENTS:
                    stage(tick - i)
        for cp in sends:
            cp.wait_send()
        gcol[c] = pack(gacc[...])
        gram = exchange(gcol, c, cols, gc_s, gc_r, lambda p: (r, p))
        upper, inverse = chol_inverse(gram)
        if last:
            core_ref[...] = upper

        @pl.loop(0, chunks)
        def _(k):
            off = pl.multiple_of(k * CHUNK, CHUNK)
            block = dot(inverse, zfull[:, pl.ds(off, CHUNK)], NN, HIGH)
            if last:
                right_ref[:, pl.ds(off, CHUNK)] = block
            else:
                put_factor(block, off)


def iterate(gradient, start, rows, cols):
    depth, n = gradient.shape
    rank, wide = start.shape
    dma = pltpu.SemaphoreType.DMA
    groups = rows // 2
    vmem = pl.BlockSpec(memory_space=pltpu.VMEM)
    return pl.pallas_call(
        functools.partial(kernel, rows, cols),
        out_shape=(
            jax.ShapeDtypeStruct((rank, depth), F32),
            jax.ShapeDtypeStruct((rank, wide), F32),
            jax.ShapeDtypeStruct((rank, rank), F32),
        ),
        in_specs=[pl.BlockSpec(memory_space=pl.ANY), vmem],
        out_specs=(vmem, vmem, vmem),
        scratch_shapes=[
            pltpu.VMEM((depth, wide), BF16),
            pltpu.VMEM((depth, wide), BF16),
            pltpu.VMEM((2, TILE, n), F32),
            pltpu.VMEM((2 * rank, wide), BF16),
            pltpu.VMEM((2 * rank, depth), BF16),
            pltpu.VMEM((depth, 2 * rank), F32),
            pltpu.VMEM((rank, depth), F32),
            pltpu.VMEM((cols - 1, rank // cols, depth), F32),
            pltpu.VMEM((rank, depth), F32),
            pltpu.VMEM((rank, wide), F32),
            pltpu.VMEM((rank // 2, wide), F32),
            pltpu.VMEM((groups - 1, rank // rows, wide), F32),
            pltpu.VMEM((rank, wide), F32),
            pltpu.VMEM((rank, rank), F32),
            pltpu.VMEM((rows, rank // 2, 2 * rank), F32),
            pltpu.VMEM((cols, rank // 2, 2 * rank), F32),
            dma((2,)),
            dma((cols - 1,)), dma((cols - 1,)), dma((cols - 1,)), dma((cols - 1,)),
            dma((rows - 1,)), dma((rows - 1,)), dma((cols - 1,)), dma((cols - 1,)),
            dma((SEGMENTS,)), dma((SEGMENTS,)),
            dma((SEGMENTS, groups - 1)), dma((SEGMENTS, groups - 1)),
            dma((SEGMENTS, groups - 1)), dma((SEGMENTS, groups - 1)),
            dma((SEGMENTS,)), dma((SEGMENTS,)),
        ],
        compiler_params=pltpu.CompilerParams(
            collective_id=0, has_side_effects=True, vmem_limit_bytes=60 * 1024 * 1024
        ),
        cost_estimate=pl.CostEstimate(flops=16 * depth * n * rank, bytes_accessed=4 * depth * n, transcendentals=0),
    )(gradient, start)


def factor_with(block, gram):
    lower = jnp.linalg.cholesky(gram)
    return (
        lax.linalg.triangular_solve(lower, block, left_side=False, lower=True, transpose_a=True),
        lower,
    )


def full_dot(a, b):
    return jnp.dot(a, b, precision=HIGH, preferred_element_type=F32)


def iterate_plain(gradient, start_block):
    omega = start_block
    for step in range(ITERS):
        ysum = lax.psum(full_dot(gradient, omega), "cols")
        left, lower_y = factor_with(ysum, lax.psum(full_dot(ysum.T, ysum), "rows"))
        zsum = lax.psum(full_dot(gradient.T, left), "rows")
        right, lower_z = factor_with(zsum, lax.psum(full_dot(zsum.T, zsum), "cols"))
        omega = right
    return left, right, lower_z


def fits(rows, cols, depth, n, rank):
    wide = -(-n // CHUNK) * CHUNK
    held = 4 * depth * wide + 4 * rank * wide * 6
    return (
        rows % 2 == 0 and rows > 2 and cols > 1 and rank % (8 * rows) == 0 and rank % (8 * cols) == 0
        and 2 * rank == 128 and depth % 128 == 0 and wide // CHUNK >= SEGMENTS and held < 50 * 1024 * 1024
    )


def per_device(rows, cols, gradient, start_block, activations, out_grads):
    depth, n = gradient.shape
    rank = start_block.shape[1]
    grad_cols = out_grads.shape[1]
    if fits(rows, cols, depth, n, rank):
        wide = -(-n // CHUNK) * CHUNK
        start = jnp.pad(start_block.T, ((0, 0), (0, wide - n)))
        left, right, upper = iterate(gradient, start, rows, cols)
        left, right, lower_z = left.T, right[:, :n].T, upper.T
    else:
        left, right, lower_z = iterate_plain(gradient, start_block)
    whole_rows = lax.all_gather(left, "rows", axis=0, tiled=True)
    left_cols = lax.dynamic_slice_in_dim(whole_rows, lax.axis_index("cols") * grad_cols, grad_cols, 0)
    token_left, token_right = lax.psum((full_dot(out_grads, left_cols), full_dot(activations, right)), "cols")
    scores = jnp.sum(full_dot(token_left, lower_z) * token_right, axis=1)
    return (left, right, scores)


def solution(mesh):
    placed = (P("rows", "cols"), P("cols", None), P("rows", "cols"), P("rows", "cols"))
    return jax.shard_map(
        functools.partial(per_device, mesh.shape["rows"], mesh.shape["cols"]),
        mesh=mesh,
        in_specs=placed,
        out_specs=(P("rows", None), P("cols", None), P("rows")),
        check_vma=False,
    )
```

time: 583 us -> 348 us (0.60)
  Pallas kernels: 0 us -> 238 us
  waiting for transfers between devices: 271 us -> 43.9 us
  matrix products: 133 us -> 5.61 us
  blocking collectives: 109 us -> 10.7 us
  other arithmetic: 48.2 us -> 0 us
  local copies, waits for them, and re-layouts: 3.03 us -> 35.2 us
    psum x4 -> x0, waiting for transfers between devices: 253 us -> none  [the longest x2 187 us: per_device(): zsum = lax.psum(partial_z, 'rows')]
    pallas_call x0 -> x1, Pallas kernels: none -> 238 us  [iterate(): pl.pallas_call(functools.partial(kernel, rows, cols), out_shape=(jax.Shap...]
    dot_general x11 -> x3, matrix products: 124 us -> 5.61 us  [full_dot(): return jnp.dot(a, b, precision=HIGH, preferred_element_type=F32)]
    psum x5 -> x1, blocking collectives: 109 us -> 10.7 us  [per_device(): lax.psum((full_dot(out_grads, left_cols), full_dot(activations, right)),...]
    another operation x20 -> x0, other arithmetic: 48.2 us -> none  [the longest x12 26.1 us: factor_with(): lower = jnp.linalg.cholesky(gram)]
    unnamed x10 -> x12, local copies, waits for them, and re-layouts: 2.73 us -> 30.9 us
    all_gather x1, waiting for transfers between devices: 17.6 us -> 43.9 us  [per_device(): whole_rows = lax.all_gather(left, 'rows', axis=0, tiled=True)]
    another operation x4 -> x0, matrix products: 9.39 us -> none  [factor_with(): lax.linalg.triangular_solve(lower, block, left_side=False, lower=True, tr...]
  transfers between devices with their start and end apart: 5 -> 1, of which waited for: 5 -> 1; matrix products, arithmetic and copies ran while one was open for 4% -> 1% of each run, Pallas kernels for 0% -> 0%
where the time goes in v1:
time: 348 us; the launch traced here: 347 us
  Pallas kernels  238 us (68%)
  waiting for transfers between devices  43.9 us (13%)
  local copies, waits for them, and re-layouts  35.2 us (10%)
  between operations  14.1 us (4%)
  blocking collectives  10.7 us (3%)
  matrix products  5.61 us (2%)
    pallas_call x1, Pallas kernels, iterate(): pl.pallas_call(functools.partial(kernel, rows, cols), out_shape=(jax.Shap...  238 us
    all_gather x1, waiting for transfers between devices, per_device(): whole_rows = lax.all_gather(left, 'rows', axis=0, tiled=True)  43.9 us
    unnamed x12, local copies, waits for them, and re-layouts  30.9 us
    psum x1, blocking collectives, per_device(): lax.psum((full_dot(out_grads, left_cols), full_dot(activations, right)),...  10.7 us
  transfers between devices with their start and end apart: 1, of which 1 were waited for; matrix products, arithmetic and copies ran while one was open for 1% of the time, Pallas kernels for 0%

profile of v1, /device:TPU:0, one launch (start us, length us, event | category | flops | bytes accessed | tf_op | source)
XLA Modules:
  0.0 347.1 jit_solution(1053383165442656689)
XLA Ops:
  7.2 0.0 copy-start
  7.2 0.0 all-gather.2.cloned.1.call-start
  7.2 30.2 %copy.7.g_ref = f32[1024,7392]{1,0:T(8,128)} copy(f32[1024,7392]{0,1:T(8,128)} %param.4) | data formatting | bytes 60555264 | tf_op args[0]
  37.4 2.9 pad.4.w0_ref
  40.3 237.6 %shard_map.67 = (f32[64,1024]{1,0:T(8,128)}, f32[64,7424]{1,0:T(8,128)}, f32[64,64]{1,0:T(8,128)}) custom-call(f32[1024,7392]{1,0:T(8,128)} %copy.7.g_ref, f32[64,7424]{1,0:T(8,128)} %pad.4.w0_ref), custom_call_target="tpu_custom_call" | custom-call | flops 7751073792 | bytes 30277632 | tf_op jit(solution)/shard_map/pallas_call | solution.py:270
  277.9 0.0 all-gather.2.cloned.1.call-update
  277.9 0.0 copy-done
  277.9 0.0 copy-start.1
  277.9 3.3 fusion.2
  281.3 0.0 copy-done.1
  281.3 0.0 copy-start.3
  281.3 0.0 copy-start.4
  281.3 0.0 copy-start.2
  281.3 1.4 slice_bitcast_fusion
  282.7 43.9 %all-gather.2.cloned.1.call-done = f32[8192,64]{0,1:T(8,128)} async-done(((f32[1024,64]{0,1:T(8,128)}), f32[8192,64]{0,1:T(8,128)}) %all-gather.2.cloned.1.call-update) | async-done | bytes 2097168 | tf_op jit(solution)/shard_map/all_gather | solution.py:354
  326.5 0.0 copy-done.3
  326.5 1.6 convolution_bitcast_fusion
  328.2 10.7 %all-reduce.1 = (f32[64,64]{0,1:T(8,128)S(1)}, f32[64,64]{0,1:T(8,128)S(1)}) all-reduce(f32[64,64]{0,1:T(8,128)S(1)} %fusion.2, f32[64,64]{0,1:T(8,128)S(1)} %convolution_bitcast_fusion), channel_id=1, replica_groups=mesh['rows'=8,'cols'=4] {'cols'}, use_global_device_ids=true, to_apply=%region_1.2 | all-reduce | flops 8192 | bytes 65536 | tf_op jit(solution)/shard_map/psum | solution.py:356
  338.9 0.0 copy-done.4
  338.9 0.7 fusion.5
  339.6 0.0 copy-done.2
  339.6 0.7 copy.9
Async XLA Ops:
  7.2 270.8 %copy-start = (f32[64,7392]{1,0:T(8,128)S(1)}, f32[64,7392]{1,0:T(8,128)}, u32[]{:S(2)}) copy-start(f32[64,7392]{1,0:T(8,128)} %param.6) | copy-start | bytes 5677060
  7.2 319.4 %all-gather.2.cloned.1.call-start = ((), (), s32[]{:S(2)}) async-start(), calls=%async_computation | async-start | bytes 2359296 | tf_op jit(solution)/shard_map/all_gather | solution.py:354
  277.9 3.3 copy-start.1
  281.3 45.3 %copy-start.3 = (f32[64,2048]{1,0:T(8,128)S(1)}, f32[64,2048]{1,0:T(8,128)}, u32[]{:S(2)}) copy-start(f32[64,2048]{1,0:T(8,128)} %param.7) | copy-start | bytes 1572868
  281.3 57.6 %copy-start.4 = (f32[64,64]{1,0:T(8,128)S(1)}, f32[64,64]{1,0:T(8,128)}, u32[]{:S(2)}) copy-start(f32[64,64]{1,0:T(8,128)} %get-tuple-element.8) | copy-start | bytes 49156
  281.3 58.3 %copy-start.2 = (f32[64,1024]{1,0:T(8,128)S(1)}, f32[64,1024]{1,0:T(8,128)}, u32[]{:S(2)}) copy-start(f32[64,1024]{1,0:T(8,128)} %get-tuple-element.6) | copy-start | bytes 786436
Sparse Core Ops, SparseCore 0:
  278.0 48.4 all-gather.1

commit v2 on v1

--- a/solution.py
+++ b/solution.py
@@ -13,7 +13,7 @@
 F32 = jnp.float32
 BF16 = jnp.bfloat16
 CHUNK = 256
-TILE = 64
+SLOTS = 4
 SEGMENTS = 7
 NT = (((1,), (1,)), ((), ()))
 NN = (((1,), (0,)), ((), ()))
@@ -54,24 +54,30 @@
 
 
 def kernel(
-    rows, cols, g_ref, w0_ref, left_ref, right_ref, core_ref,
-    ghi, glo, fbuf, wcat, lcat, acc, ypart, yrecv, yfull, zpart, zpair, zgroup, zfull, gacc, grow, gcol,
-    load_sem, ys_s, ys_r, ya_s, ya_r, gr_s, gr_r, gc_s, gc_r, p_s, p_r, q_s, q_r, a_s, a_r, b_s, b_r,
+    rows, cols, g_ref, w0_ref, act_ref, og_ref, left_ref, right_ref, score_ref,
+    ghi, glo, fbuf, ftail, wcat, lcat, acc, ypart, yrecv, yfull, zpart, zpair, zgroup, zfull, gacc, grow, gcol, lsel, tok,
+    load_sem, tail_sem, ys_s, ys_r, ya_s, ya_r, gr_s, gr_r, gc_s, gc_r, p_s, p_r, q_s, q_r, a_s, a_r, b_s, b_r,
+    l_s, l_r, m_s, m_r, t_s, t_r,
 ):
     r, c = lax.axis_index("rows"), lax.axis_index("cols")
     rank, wide = zfull.shape
-    depth, n = g_ref.shape
+    n, depth = g_ref.shape
     groups = rows // 2
     y, q = lax.rem(r, 2), lax.div(r, 2)
     half, eighth, quarter = rank // 2, rank // rows, rank // cols
-    chunks = wide // CHUNK
-
-    def load(t, slot):
-        return pltpu.make_async_copy(
-            g_ref.at[pl.ds(pl.multiple_of(t * TILE, TILE), TILE), :], fbuf.at[slot], load_sem.at[slot]
-        )
-
-    load(0, 0).start()
+    chunks, full = wide // CHUNK, n // CHUNK
+    cut, rest = full * CHUNK, n - full * CHUNK
+
+    def load(k):
+        slot = lax.rem(k, SLOTS)
+        at = pl.ds(pl.multiple_of(k * CHUNK, CHUNK), CHUNK)
+        return pltpu.make_async_copy(g_ref.at[at, :], fbuf.at[slot], load_sem.at[slot])
+
+    for k in range(SLOTS):
+        load(k).start()
+    if rest:
+        load_tail = pltpu.make_async_copy(g_ref.at[cut:n, :], ftail, tail_sem.at[0])
+        load_tail.start()
 
     barrier = pltpu.get_barrier_semaphore()
     for d in range(1, rows):
@@ -84,28 +90,41 @@
         wcat[:rank, pl.ds(off, CHUNK)] = hi
         wcat[rank:, pl.ds(off, CHUNK)] = lo
 
-    @pl.loop(0, chunks)
+    def times(k):
+        at = pl.ds(pl.multiple_of(k * CHUNK, CHUNK), CHUNK)
+        w = wcat[:, at]
+        acc[...] += dot(w, ghi[at, :], NN) + dot(w, glo[at, :], NN)
+
+    acc[...] = jnp.zeros_like(acc)
+
+    @pl.loop(0, full)
     def _(k):
+        slot = lax.rem(k, SLOTS)
         off = pl.multiple_of(k * CHUNK, CHUNK)
         put_factor(w0_ref[:, pl.ds(off, CHUNK)], off)
-
-    ghi[:, wide - CHUNK :] = jnp.zeros((depth, CHUNK), BF16)
-    glo[:, wide - CHUNK :] = jnp.zeros((depth, CHUNK), BF16)
-    tiles = depth // TILE
-
-    @pl.loop(0, tiles)
-    def _(t):
-        slot = lax.rem(t, 2)
-        load(t, slot).wait()
-
-        @pl.when(t + 1 < tiles)
+        load(k).wait()
+        hi, lo = split(fbuf[slot])
+        ghi[pl.ds(off, CHUNK), :] = hi
+        glo[pl.ds(off, CHUNK), :] = lo
+
+        @pl.when(k + SLOTS < full)
         def _():
-            load(t + 1, 1 - slot).start()
-
-        hi, lo = split(fbuf[slot])
-        at = pl.ds(pl.multiple_of(t * TILE, TILE), TILE)
-        ghi[at, :n] = hi
-        glo[at, :n] = lo
+            load(k + SLOTS).start()
+
+        times(k)
+
+    if rest:
+        wcat[:, cut:] = jnp.zeros((2 * rank, CHUNK), BF16)
+        ghi[cut:, :] = jnp.zeros((CHUNK, depth), BF16)
+        glo[cut:, :] = jnp.zeros((CHUNK, depth), BF16)
+        hi, lo = split(w0_ref[:, cut:n])
+        wcat[:rank, cut:n] = hi
+        wcat[rank:, cut:n] = lo
+        load_tail.wait()
+        hi, lo = split(ftail[...])
+        ghi[cut:n, :] = hi
+        glo[cut:n, :] = lo
+        times(full)
 
     pl.semaphore_wait(barrier, rows + cols - 2)
 
@@ -125,7 +144,7 @@
         total = slots[0]
         for i in range(1, count):
             total = total + slots[i]
-        return unpack(total)
+        return total
 
     def rows_at(start, size):
         return pl.ds(pl.multiple_of(start, 8), size)
@@ -134,17 +153,10 @@
 
     for step in range(ITERS):
         last = step == ITERS - 1
-        acc[...] = jnp.zeros_like(acc)
-
-        @pl.loop(0, chunks)
-        def _(k):
-            at = pl.ds(pl.multiple_of(k * CHUNK, CHUNK), CHUNK)
-            w = wcat[:, at]
-            acc[...] += dot(ghi[:, at], w, NT) + dot(glo[:, at], w, NT)
-
-        for i in range(0, depth, 128):
-            turned = acc[i : i + 128, :].T
-            ypart[:, i : i + 128] = turned[:rank] + turned[rank:]
+        if step:
+            acc[...] = jnp.zeros_like(acc)
+            pl.loop(0, chunks)(times)
+        ypart[...] = acc[:rank, :] + acc[rank:, :]
         cps = []
         for d in range(1, cols):
             p = lax.rem(c + d, cols)
@@ -163,11 +175,15 @@
         for cp in cps:
             cp.wait()
         grow[r] = pack(dot(yfull[...], yfull[...], NT, HIGH))
-        gram = exchange(grow, r, rows, gr_s, gr_r, lambda p: (p, c))
+        gram = unpack(exchange(grow, r, rows, gr_s, gr_r, lambda p: (p, c)))
         _, inverse = chol_inverse(gram)
         left = dot(inverse, yfull[...], NN, HIGH)
         if last:
             left_ref[...] = left
+
+            @pl.when(q == c)
+            def _():
+                lsel[y] = left
         hi, lo = split(left)
         lcat[:rank, :] = hi
         lcat[rank:, :] = lo
@@ -191,7 +207,7 @@
             @pl.loop(bounds[s], bounds[s + 1])
             def _(k):
                 at = pl.ds(pl.multiple_of(k * CHUNK, CHUNK), CHUNK)
-                part = dot(lcat[...], ghi[:, at], NN) + dot(lcat[...], glo[:, at], NN)
+                part = (dot(ghi[at, :], lcat[...], NT) + dot(glo[at, :], lcat[...], NT)).T
                 zpart[:, at] = part[:rank] + part[rank:]
 
             other = rows_at((1 - y) * half, half)
@@ -245,25 +261,64 @@
                     stage(tick - i)
         for cp in sends:
             cp.wait_send()
+        if last:
+            def spread(d):
+                return pltpu.make_async_remote_copy(
+                    src_ref=left_ref, dst_ref=lsel.at[y], send_sem=l_s.at[d - 1], recv_sem=l_r.at[0],
+                    device_id=(2 * lax.rem(q + d, groups) + y, c), device_id_type=MESH,
+                )
+
+            @pl.when(q == c)
+            def _():
+                for d in range(1, groups):
+                    spread(d).start()
         gcol[c] = pack(gacc[...])
-        gram = exchange(gcol, c, cols, gc_s, gc_r, lambda p: (r, p))
+        gram = unpack(exchange(gcol, c, cols, gc_s, gc_r, lambda p: (r, p)))
         upper, inverse = chol_inverse(gram)
-        if last:
-            core_ref[...] = upper
-
-        @pl.loop(0, chunks)
-        def _(k):
-            off = pl.multiple_of(k * CHUNK, CHUNK)
-            block = dot(inverse, zfull[:, pl.ds(off, CHUNK)], NN, HIGH)
-            if last:
-                right_ref[:, pl.ds(off, CHUNK)] = block
-            else:
-                put_factor(block, off)
-
-
-def iterate(gradient, start, rows, cols):
-    depth, n = gradient.shape
-    rank, wide = start.shape
+        if not last:
+
+            @pl.loop(0, chunks)
+            def _(k):
+                off = pl.multiple_of(k * CHUNK, CHUNK)
+                put_factor(dot(inverse, zfull[:, pl.ds(off, CHUNK)], NN, HIGH), off)
+
+    @pl.when(q != c)
+    def _():
+        spread(1).wait_recv()
+
+    swap = copy(lsel.at[y], lsel.at[y], m_s.at[0], m_r.at[0], pair)
+    gacc[...] = jnp.zeros_like(gacc)
+
+    @pl.loop(0, full)
+    def _(k):
+        at = pl.ds(pl.multiple_of(k * CHUNK, CHUNK), CHUNK)
+        block = dot(inverse, zfull[:, at], NN, HIGH)
+        right_ref[:, at] = block
+        gacc[...] += dot(act_ref[:, at], block, NT, HIGH)
+
+    if rest:
+        block = dot(inverse, zfull[:, cut:], NN, HIGH)[:, :rest]
+        right_ref[:, cut:n] = block
+        gacc[...] += dot(act_ref[:, cut:n], block, NT, HIGH)
+    swap.wait()
+
+    @pl.when(q == c)
+    def _():
+        for d in range(1, groups):
+            spread(d).wait_send()
+
+    token_left = dot(og_ref[:, :depth], lsel[0], NT, HIGH) + dot(og_ref[:, depth:], lsel[1], NT, HIGH)
+    tok[c] = jnp.concatenate([token_left, gacc[...]], axis=1)
+    tokens = exchange(tok, c, cols, t_s, t_r, lambda p: (r, p))
+    mixed = dot(tokens[:, :rank], upper, NT, HIGH)
+    score_ref[...] = dot(jnp.ones((8, rank), F32), mixed * tokens[:, rank:], NT, HIGH)
+
+
+def iterate(gradient, start, activations, out_grads, rows, cols):
+    n, depth = gradient.shape
+    rank = start.shape[0]
+    tokens = activations.shape[0]
+    wide = -(-n // CHUNK) * CHUNK
     dma = pltpu.SemaphoreType.DMA
     groups = rows // 2
     vmem = pl.BlockSpec(memory_space=pltpu.VMEM)
@@ -271,18 +326,19 @@
         functools.partial(kernel, rows, cols),
         out_shape=(
             jax.ShapeDtypeStruct((rank, depth), F32),
-            jax.ShapeDtypeStruct((rank, wide), F32),
-            jax.ShapeDtypeStruct((rank, rank), F32),
+            jax.ShapeDtypeStruct((rank, n), F32),
+            jax.ShapeDtypeStruct((8, tokens), F32),
         ),
-        in_specs=[pl.BlockSpec(memory_space=pl.ANY), vmem],
+        in_specs=[pl.BlockSpec(memory_space=pl.ANY), vmem, vmem, vmem],
         out_specs=(vmem, vmem, vmem),
         scratch_shapes=[
-            pltpu.VMEM((depth, wide), BF16),
-            pltpu.VMEM((depth, wide), BF16),
-            pltpu.VMEM((2, TILE, n), F32),
+            pltpu.VMEM((wide, depth), BF16),
+            pltpu.VMEM((wide, depth), BF16),
+            pltpu.VMEM((SLOTS, CHUNK, depth), F32),
+            pltpu.VMEM((n % CHUNK or 8, depth), F32),
             pltpu.VMEM((2 * rank, wide), BF16),
             pltpu.VMEM((2 * rank, depth), BF16),
-            pltpu.VMEM((depth, 2 * rank), F32),
+            pltpu.VMEM((2 * rank, depth), F32),
             pltpu.VMEM((rank, depth), F32),
             pltpu.VMEM((cols - 1, rank // cols, depth), F32),
             pltpu.VMEM((rank, depth), F32),
@@ -293,19 +349,22 @@
             pltpu.VMEM((rank, rank), F32),
             pltpu.VMEM((rows, rank // 2, 2 * rank), F32),
             pltpu.VMEM((cols, rank // 2, 2 * rank), F32),
-            dma((2,)),
+            pltpu.VMEM((2, rank, depth), F32),
+            pltpu.VMEM((cols, tokens, 2 * rank), F32),
+            dma((SLOTS,)), dma((1,)),
             dma((cols - 1,)), dma((cols - 1,)), dma((cols - 1,)), dma((cols - 1,)),
             dma((rows - 1,)), dma((rows - 1,)), dma((cols - 1,)), dma((cols - 1,)),
             dma((SEGMENTS,)), dma((SEGMENTS,)),
             dma((SEGMENTS, groups - 1)), dma((SEGMENTS, groups - 1)),
             dma((SEGMENTS, groups - 1)), dma((SEGMENTS, groups - 1)),
             dma((SEGMENTS,)), dma((SEGMENTS,)),
+            dma((groups - 1,)), dma((1,)), dma((1,)), dma((1,)), dma((cols - 1,)), dma((cols - 1,)),
         ],
         compiler_params=pltpu.CompilerParams(
-            collective_id=0, has_side_effects=True, vmem_limit_bytes=60 * 1024 * 1024
+            collective_id=0, has_side_effects=True, vmem_limit_bytes=63 * 1024 * 1024
         ),
         cost_estimate=pl.CostEstimate(flops=16 * depth * n * rank, bytes_accessed=4 * depth * n, transcendentals=0),
-    )(gradient, start)
+    )(gradient, start, activations, out_grads)
 
 
 def factor_with(block, gram):
@@ -331,26 +390,24 @@
     return left, right, lower_z
 
 
-def fits(rows, cols, depth, n, rank):
+def fits(rows, cols, depth, n, rank, tokens, grad_cols):
     wide = -(-n // CHUNK) * CHUNK
-    held = 4 * depth * wide + 4 * rank * wide * 6
+    held = 4 * depth * wide + 4 * rank * wide * 7
     return (
-        rows % 2 == 0 and rows > 2 and cols > 1 and rank % (8 * rows) == 0 and rank % (8 * cols) == 0
-        and 2 * rank == 128 and depth % 128 == 0 and wide // CHUNK >= SEGMENTS and held < 50 * 1024 * 1024
+        rows == 2 * cols and cols > 1 and rank % (8 * rows) == 0 and 2 * rank == 128 and depth % 128 == 0
+        and n % 16 == 0 and n // CHUNK >= max(SEGMENTS, SLOTS) and held < 50 * 1024 * 1024
+        and grad_cols == 2 * depth and tokens % 8 == 0 and tokens <= 128
     )
 
 
 def per_device(rows, cols, gradient, start_block, activations, out_grads):
     depth, n = gradient.shape
     rank = start_block.shape[1]
-    grad_cols = out_grads.shape[1]
-    if fits(rows, cols, depth, n, rank):
-        wide = -(-n // CHUNK) * CHUNK
-        start = jnp.pad(start_block.T, ((0, 0), (0, wide - n)))
-        left, right, upper = iterate(gradient, start, rows, cols)
-        left, right, lower_z = left.T, right[:, :n].T, upper.T
-    else:
-        left, right, lower_z = iterate_plain(gradient, start_block)
+    tokens, grad_cols = out_grads.shape
+    if fits(rows, cols, depth, n, rank, tokens, grad_cols):
+        left, right, scores = iterate(gradient.T, start_block.T, activations, out_grads, rows, cols)
+        return left.T, right.T, scores[0]
+    left, right, lower_z = iterate_plain(gradient, start_block)
     whole_rows = lax.all_gather(left, "rows", axis=0, tiled=True)
     left_cols = lax.dynamic_slice_in_dim(whole_rows, lax.axis_index("cols") * grad_cols, grad_cols, 0)
     token_left, token_right = lax.psum((full_dot(out_grads, left_cols), full_dot(activations, right)), "cols")

time: 348 us -> 232 us (0.67)
  waiting for transfers between devices: 43.9 us -> 0 us
  local copies, waits for them, and re-layouts: 35.2 us -> 5.75 us
  between operations: 14.1 us -> 0.64 us
  Pallas kernels: 238 us -> 225 us
  blocking collectives: 10.7 us -> 0 us
  matrix products: 5.61 us -> 0 us
    all_gather x1 -> x0, waiting for transfers between devices: 43.9 us -> none  [per_device(): whole_rows = lax.all_gather(left, 'rows', axis=0, tiled=True)]
    unnamed x12 -> x2, local copies, waits for them, and re-layouts: 30.9 us -> 4.56 us
    pallas_call x1, Pallas kernels: 238 us -> 225 us  [iterate(): pl.pallas_call(functools.partial(kernel, rows, cols), out_shape=(jax.Shap...]
    psum x1 -> x0, blocking collectives: 10.7 us -> none  [per_device(): lax.psum((full_dot(out_grads, left_cols), full_dot(activations, right)),...]
    dot_general x3 -> x0, matrix products: 5.61 us -> none  [full_dot(): return jnp.dot(a, b, precision=HIGH, preferred_element_type=F32)]
  transfers between devices with their start and end apart: 1 -> 0, of which waited for: 1 -> 0; matrix products, arithmetic and copies ran while one was open for 1% -> 0% of each run, Pallas kernels for 0% -> 0%
where the time goes in v2:
time: 232 us; the launch traced here: 231 us
  Pallas kernels  225 us (97%)
  local copies, waits for them, and re-layouts  5.75 us (2%)
    pallas_call x1, Pallas kernels, iterate(): pl.pallas_call(functools.partial(kernel, rows, cols), out_shape=(jax.Shap...  225 us

profile of v2, /device:TPU:0, one launch (start us, length us, event | category | flops | bytes accessed | tf_op | source)
XLA Modules:
  0.0 231.1 jit_solution(15333165217668603005)
XLA Ops:
  0.6 224.7 %shard_map.67 = (f32[64,1024]{1,0:T(8,128)}, f32[64,7392]{1,0:T(8,128)}, f32[8,64]{1,0:T(8,128)}) custom-call(f32[7392,1024]{1,0:T(8,128)} %bitcast.6, f32[64,7392]{1,0:T(8,128)} %bitcast.8, f32[64,7392]{1,0:T(8,128)} %act_ref.1, f32[64,2048]{1,0:T(8,128)} %og_ref.1), custom_call_target="tpu_custom_call" | custom-call | flops 7751073792 | bytes 30277632 | tf_op jit(solution)/shard_map/pallas_call | solution.py:325
  225.4 1.2 slice_bitcast_fusion
  226.6 1.7 copy.9
  228.2 2.9 %copy.10 = f32[7392,64]{0,1:T(8,128)} copy(f32[7392,64]{0,1:T(8,128)} %bitcast.7) | data formatting | bytes 3784704

commit v3 on v2

--- a/solution.py
+++ b/solution.py
@@ -34,10 +34,16 @@
     lane = lax.broadcasted_iota(jnp.int32, (n, 2 * n), 1)
     eye = (lax.broadcasted_iota(jnp.int32, (n, n), 0) == lax.broadcasted_iota(jnp.int32, (n, n), 1)).astype(F32)
     w = jnp.concatenate([gram, eye], axis=1)
-    for k in range(n):
-        row = w[k : k + 1, :]
-        scaled = row * (1.0 / row[:, k : k + 1])
-        w = w - jnp.where(sub > k, w[:, k : k + 1], 0.0) * scaled
+    for k in range(0, n, 2):
+        row0, row1 = w[k : k + 1, :], w[k + 1 : k + 2, :]
+        col0, col1 = w[:, k : k + 1], w[:, k + 1 : k + 2]
+        inv0 = 1.0 / row0[:, k : k + 1]
+        scaled0 = row0 * inv0
+        below = row1[:, k : k + 1]
+        across = row0[:, k + 1 : k + 2] * inv0
+        inv1 = 1.0 / (row1[:, k + 1 : k + 2] - below * across)
+        scaled1 = (row1 - below * scaled0) * inv1
+        w = w - jnp.where(sub > k, col0, 0.0) * scaled0 - jnp.where(sub > k + 1, col1 - col0 * across, 0.0) * scaled1
     diag = jnp.sum(jnp.where(sub == lane, w, 0.0), axis=1, keepdims=True)
     w = w * (1.0 / jnp.sqrt(diag))
     return w[:, :n], w[:, n:]

time: 232 us -> 247 us (1.065)
  Pallas kernels: 225 us -> 240 us
    pallas_call x1, Pallas kernels: 225 us -> 240 us  [iterate(): pl.pallas_call(functools.partial(kernel, rows, cols), out_shape=(jax.Shap...]
where the time goes in v3:
time: 247 us
  Pallas kernels  240 us (97%)
  local copies, waits for them, and re-layouts  5.75 us (2%)
    pallas_call x1, Pallas kernels, iterate(): pl.pallas_call(functools.partial(kernel, rows, cols), out_shape=(jax.Shap...  240 us

profile of v3, /device:TPU:0, one launch (start us, length us, event | category | flops | bytes accessed | tf_op | source)
XLA Modules:
  0.0 246.6 jit_solution(615782777774808965)
XLA Ops:
  0.6 240.3 %shard_map.67 = (f32[64,1024]{1,0:T(8,128)}, f32[64,7392]{1,0:T(8,128)}, f32[8,64]{1,0:T(8,128)}) custom-call(f32[7392,1024]{1,0:T(8,128)} %bitcast.6, f32[64,7392]{1,0:T(8,128)} %bitcast.8, f32[64,7392]{1,0:T(8,128)} %act_ref.1, f32[64,2048]{1,0:T(8,128)} %og_ref.1), custom_call_target="tpu_custom_call" | custom-call | flops 7751073792 | bytes 30277632 | tf_op jit(solution)/shard_map/pallas_call | solution.py:331
  240.9 1.2 slice_bitcast_fusion
  242.1 1.7 copy.9
  243.7 2.9 %copy.10 = f32[7392,64]{0,1:T(8,128)} copy(f32[7392,64]{0,1:T(8,128)} %bitcast.7) | data formatting | bytes 3784704
